TPU v7x, 32 devices: a whole 2x2x4 slice. The times are simulated.
32 devices in a mesh: scan: 2 (over y), angle: 16 (over z, x, core).
Axes of the slice: x: 2, y: 2, z: 4, core: 2. Of those that a mesh axis runs over, the one named last changes fastest.
Arguments:
- object_init: float32 [32, 2, 128, 1024], P(('scan', 'angle')), parts along dimension 0, may hold values from -3.6 to 3.6
- measured: bfloat16 [32, 15, 128, 128], P(('scan', 'angle')), parts along dimension 0
- positions: int32 [32, 15, 2], P(('scan', 'angle')), parts along dimension 0, may hold values from 0 to 896, as said below
- angle_list: int32 [32], P('scan'), parts along dimension 0, may hold values from 0 to 15, each once
- probe: float32 [4, 128, 128], P('scan'), parts along dimension 0, may hold values from -3 to 3
- radial: float32 [16, 1024, 1024], P('angle'), may hold values from -0.1875 to 0.1875
Outputs:
- slices: float32 [32, 2, 128, 1024], P(('scan', 'angle')), parts along dimension 0
- probe_out: float32 [4, 128, 128], P('scan'), parts along dimension 0
There are 2 independent parts, one for each index of `scan`. A program takes and returns all parts, laid end to end along the dimension named above; an argument that names none is the same for every part. Nothing has to cross between parts.
Inputs may be any that keep to these rules, and one draw needn't show every extreme that they name: `positions`: for each angle, patch number n = r * 15 + c has offsets (r * 64, c * 64) moved by at most 8 cells in each dimension and clipped so that the patch lies inside the 128 x 1024 projection.
All inputs are finite; a program needn't handle non-finite values.
Results may differ from a plain program's by a relative error of at most 0.0014.
The roundings to bfloat16 on the way count: a program that leaves them out, or rounds other values in their place, can miss the bound.
Values sent between devices are 32-bit elements; how exact they have to be, the bound alone decides.
A program may use at most 64 MiB of HBM per device.

v0:
```python
import functools
import math

import jax
import jax.numpy as jnp
import numpy as np
from jax import lax
from jax.experimental import pallas as pl
from jax.experimental.pallas import tpu as pltpu
from jax.sharding import PartitionSpec as P

ITERS = 2
CHUNKS = 4
LANES = 128
SUBLANES = 8

object_rate = 0.5
probe_rate = 1.0

VMEM_SPEC = pl.BlockSpec(memory_space=pltpu.VMEM)
SMEM_SPEC = pl.BlockSpec(memory_space=pltpu.SMEM)
ANY_SPEC = pl.BlockSpec(memory_space=pl.ANY)


def tables_exact(count, index_list):
    index = jnp.arange(count, dtype=jnp.int32)
    phase = index[:, None] * index_list[None, :] % count
    angle = phase.astype(jnp.float32) * (2.0 * math.pi / count)
    scale = 1.0 / math.sqrt(count)
    return (jnp.cos(angle) * scale, jnp.sin(angle) * scale)


def block_tables(count):
    index = np.arange(count)
    phase = index[:, None] * index[None, :] % count
    angle = phase.astype(np.float32) * np.float32(2.0 * math.pi / count)
    scale = np.float32(1.0 / math.sqrt(count))
    cosine, sine = np.cos(angle) * scale, np.sin(angle) * scale
    forward = np.block([[cosine, sine], [-sine, cosine]]).astype(jnp.bfloat16)
    inverse = np.block([[cosine, -sine], [sine, cosine]]).astype(jnp.bfloat16)
    return forward, inverse


def dot32(a, b):
    return jnp.dot(a, b, preferred_element_type=jnp.float32)


def greet(n, me):
    barrier = pltpu.get_barrier_semaphore()

    def one(i, carry):
        pl.semaphore_signal(
            barrier, inc=1, device_id={"angle": lax.rem(me + i, n)},
            device_id_type=pl.DeviceIdType.MESH,
        )
        return carry

    lax.fori_loop(1, n, one, 0)


def send(n, me, make):
    def one(i, carry):
        d = lax.rem(me + i, n)
        src, dst, send_sem, recv_sem = make(d)
        pltpu.make_async_remote_copy(
            src_ref=src, dst_ref=dst, send_sem=send_sem, recv_sem=recv_sem,
            device_id={"angle": d}, device_id_type=pl.DeviceIdType.MESH,
        ).start()
        return carry

    lax.fori_loop(1, n, one, 0)


def drain(ref, sem):
    pltpu.make_async_copy(ref, ref, sem).wait()


def rows_at(d, count):
    return pl.ds(pl.multiple_of(d * count, SUBLANES), count)


def gradient_pass(span, place, obj, meas, probe, fwd_ref, inv_ref, pg, acc, energy, piece, wave, mid, first):
    size = wave.shape[0] // 2
    rows = obj.shape[1]
    tiles = obj.shape[2] // size
    lane = lax.broadcasted_iota(jnp.int32, (rows, size), 1)
    probe_re, probe_im = probe[:size, :], probe[size:, :]
    numbers = range(*span)
    at = {n: i for i, n in enumerate(numbers)}
    tile = lambda ref, c, t: ref[c, :, t * size:(t + 1) * size]

    for n in numbers:
        i = at[n]
        col, turn, low = place(n)
        keep = lane < size - turn
        parts = []
        for c in range(2):
            if 2 * low == n and low > 0:
                before = jnp.full((rows, size), col, jnp.int32) < low * size
                left = jnp.where(before, tile(obj, c, low - 1), tile(obj, c, low))
                right = jnp.where(before, tile(obj, c, low), tile(obj, c, min(low + 1, tiles - 1)))
            else:
                left, right = tile(obj, c, low), tile(obj, c, min(low + 1, tiles - 1))
            back = lax.rem(size - turn, size)
            parts.append(jnp.where(keep, pltpu.roll(left, back, 1), pltpu.roll(right, back, 1)))
        p_re, p_im = parts
        piece[i, 0] = p_re
        piece[i, 1] = p_im
        energy += jnp.sum((p_re * p_re + p_im * p_im).reshape(-1, SUBLANES, size), 0)
        wave[:size, i * size:(i + 1) * size] = (probe_re * p_re - probe_im * p_im).astype(jnp.bfloat16)
        wave[size:, i * size:(i + 1) * size] = (probe_re * p_im + probe_im * p_re).astype(jnp.bfloat16)

    def left_product(table_ref):
        for i in range(0, len(numbers), 2):
            many = min(2, len(numbers) - i)
            got = dot32(table_ref[...], wave[:, i * size:(i + many) * size]).astype(jnp.bfloat16)
            for j in range(many):
                part = slice((i + j) * size, (i + j + 1) * size)
                mid[part, :size] = got[:size, j * size:(j + 1) * size]
                mid[part, size:] = got[size:, j * size:(j + 1) * size]

    left_product(fwd_ref)
    for n in numbers:
        part = slice(at[n] * size, (at[n] + 1) * size)
        far = dot32(mid[part, :], inv_ref[...])
        far_re, far_im = far[:, :size], far[:, size:]
        resid = far_re * far_re + far_im * far_im - meas[n].astype(jnp.float32)
        wave[:size, part] = (resid * far_re).astype(jnp.bfloat16)
        wave[size:, part] = (resid * far_im).astype(jnp.bfloat16)
    left_product(inv_ref)
    for n in numbers:
        i = at[n]
        col, turn, low = place(n)
        grad = dot32(mid[i * size:(i + 1) * size, :], fwd_ref[...])
        g_re, g_im = grad[:, :size], grad[:, size:]
        p_re, p_im = piece[i, 0], piece[i, 1]
        pg_re = p_re * g_re + p_im * g_im
        pg_im = p_re * g_im - p_im * g_re
        if first and i == 0:
            pg[:size, :], pg[size:, :] = pg_re, pg_im
        else:
            pg[:size, :] += pg_re
            pg[size:, :] += pg_im
        steps = (probe_re * g_re + probe_im * g_im, probe_re * g_im - probe_im * g_re)
        ends = [low, low + 1] if 2 * low < n or low == 0 else [low - 1, low, low + 1]
        for c in range(2):
            turned = pltpu.roll(steps[c], turn, 1)
            for t in ends:
                if t < tiles:
                    where = lane + t * size
                    inside = (where >= col) & (where < col + size)
                    acc[c, :, t * size:(t + 1) * size] += jnp.where(inside, turned, 0.0)
    return energy


class Reduction:
    def __init__(self, n, me, pg, en, got_pg, got_en, full, sems):
        self.n, self.me, self.pg, self.en = n, me, pg, en
        self.got_pg, self.got_en, self.full, self.sems = got_pg, got_en, full, sems
        self.share = pg.shape[0] // n

    @staticmethod
    def scratch(n, rows, size):
        return [
            pltpu.VMEM((rows, size), jnp.float32),
            pltpu.VMEM((1, size), jnp.float32),
            pltpu.VMEM((n, rows // n, size), jnp.float32),
            pltpu.VMEM((n, 1, size), jnp.float32),
            pltpu.VMEM((rows, size), jnp.float32),
            pltpu.SemaphoreType.DMA((6,)),
        ]

    def scatter(self):
        n, me, sems = self.n, self.me, self.sems
        send(n, me, lambda d: (self.en, self.got_en.at[me], sems.at[2], sems.at[3]))
        send(n, me, lambda d: (self.pg.at[rows_at(d, self.share)], self.got_pg.at[me], sems.at[0], sems.at[1]))
        self.got_pg[me] = self.pg[rows_at(me, self.share), :]
        self.got_en[me] = self.en[...]

    def gather(self, probe):
        n, me, sems = self.n, self.me, self.sems
        drain(self.got_pg.at[pl.ds(0, n - 1)], sems.at[1])
        drain(self.got_en.at[pl.ds(0, n - 1)], sems.at[3])
        size = probe.shape[1]
        total = jnp.sum(self.got_pg[...], 0)
        energy = jnp.sum(self.got_en[...])
        mine = rows_at(me, self.share)
        self.full[mine, :] = probe[mine, :] - probe_rate * total / (energy / (size * size))
        send(n, me, lambda d: (self.full.at[mine], self.full.at[mine], sems.at[4], sems.at[5]))

    def arrive(self):
        drain(self.full.at[pl.ds(0, (self.n - 1) * self.share)], self.sems.at[5])

    def leave(self):
        sems, n = self.sems, self.n
        drain(self.got_pg.at[pl.ds(0, n - 1)], sems.at[0])
        drain(self.got_en.at[pl.ds(0, n - 1)], sems.at[2])
        drain(self.full.at[pl.ds(0, (n - 1) * self.share)], sems.at[4])


def whole_kernel(
    n, pos_ref, ang_ref, obj_hbm, meas_hbm, prb_hbm, fwd_hbm, inv_hbm, radial_hbm, cos_ref, sin_ref,
    out_ref, probe_ref,
    obj, meas, prb, fwd, inv, acc, piece, wave, mid,
    got, spread, harm, matrix, load_sems, send_a, recv_a, send_b, recv_b, *reds,
):
    me = lax.axis_index("angle")
    rows, cols = obj.shape[1:]
    patches, size = meas.shape[0], meas.shape[1]
    share, wide = rows // n, cols // CHUNKS
    loads = [
        pltpu.make_async_copy(src, dst, load_sems.at[i])
        for i, (src, dst) in enumerate((
            (obj_hbm, obj), (prb_hbm, prb), (fwd_hbm, fwd), (inv_hbm, inv), (meas_hbm, meas), (radial_hbm, matrix),
        ))
    ]
    for load in loads:
        load.start()
    greet(n, me)
    acc[...] = jnp.zeros_like(acc)
    for load in loads[:-1]:
        load.wait()

    def place(k):
        col = pos_ref[0, k, 1]
        return col, lax.rem(col, size), k // 2

    spans = [pl.ds(q * wide, wide) for q in range(CHUNKS)]
    ends = [min(patches, 2 * (wide // size) * (q + 1) + 1) for q in range(CHUNKS)]
    groups = list(zip([0] + ends[:-1], ends))
    each = len(reds) // ITERS
    probe = prb
    for step in range(ITERS):
        red = Reduction(n, me, *reds[step * each:(step + 1) * each])
        pre, pim = probe[:size, :], probe[size:, :]
        rate = object_rate / jnp.max(pre * pre + pim * pim)
        energy = jnp.zeros((SUBLANES, size), jnp.float32)
        for q, group in enumerate(groups):
            energy = gradient_pass(
                group, place, obj, meas, probe, fwd, inv, red.pg, acc, energy, piece, wave, mid, q == 0
            )
            span = spans[q]
            obj[:, :, span] = obj[:, :, span] - rate * acc[:, :, span]
            acc[:, :, span] = jnp.zeros((2, rows, wide), jnp.float32)
            if step == ITERS - 1:
                send(n, me, lambda d: (
                    obj.at[:, rows_at(d, share), span], got.at[me, :, :, span], send_a.at[q], recv_a.at[q]
                ))
        red.en[...] = jnp.sum(energy, 0, keepdims=True)
        if step == 0:
            pl.semaphore_wait(pltpu.get_barrier_semaphore(), n - 1)
        red.scatter()
        if step < ITERS - 1:
            red.gather(probe)
            red.arrive()
            red.leave()
            probe = red.full
    got[me] = obj[:, rows_at(me, share), :]
    red.gather(probe)

    def weight(ref, k, b):
        return ref[lax.rem(k * ang_ref[b], n)]

    for q, span in enumerate(spans):
        drain(got.at[pl.ds(0, n - 1), :, :, span], recv_a.at[q])

        def harmonic(k, carry):
            re = jnp.zeros((share, wide), jnp.float32)
            im = jnp.zeros((share, wide), jnp.float32)
            for b in range(n):
                wc, ws = weight(cos_ref, k, b), weight(sin_ref, k, b)
                pr, pi = got[b, 0, :, span], got[b, 1, :, span]
                re += wc * pr + ws * pi
                im += wc * pi - ws * pr
            spread[k, 0, :, span] = re
            spread[k, 1, :, span] = im
            return carry

        lax.fori_loop(0, n, harmonic, 0)
        send(n, me, lambda d: (
            spread.at[d, :, :, span], harm.at[:, rows_at(me, share), span], send_b.at[q], recv_b.at[q]
        ))
        harm[:, rows_at(me, share), span] = spread[me, :, :, span]
    loads[-1].wait()
    for q, span in enumerate(spans):
        drain(harm.at[:, pl.ds(0, (n - 1) * share), span], recv_b.at[q])
        part = jnp.dot(
            harm[:, :, span].reshape(2 * rows, wide), matrix[span, :],
            precision=lax.Precision.HIGHEST, preferred_element_type=jnp.float32,
        )
        if q == 0:
            out_ref[...] = part
        else:
            out_ref[...] += part
        if q == CHUNKS - 2:
            red.arrive()
            probe_ref[...] = red.full[...]
    red.leave()
    for q, span in enumerate(spans):
        drain(got.at[pl.ds(0, n - 1), :, :, span], send_a.at[q])
        drain(got.at[pl.ds(0, n - 1), :, :, span], send_b.at[q])


def whole_call(n, object_init, measured, positions, angle_list, probe, radial):
    rows, cols = object_init.shape[2:]
    patches, size = measured.shape[1:3]
    prows = 2 * size
    f32, bf16 = jnp.float32, jnp.bfloat16
    forward, inverse = block_tables(size)
    phase = np.arange(n).astype(np.float32) * np.float32(2.0 * math.pi / n)
    scale = np.float32(1.0 / math.sqrt(n))
    slices, probe_out = pl.pallas_call(
        functools.partial(whole_kernel, n),
        name="whole",
        out_shape=(
            jax.ShapeDtypeStruct((2 * rows, cols), f32),
            jax.ShapeDtypeStruct((prows, size), f32),
        ),
        in_specs=[SMEM_SPEC] * 2 + [ANY_SPEC] * 6 + [SMEM_SPEC] * 2,
        out_specs=(VMEM_SPEC,) * 2,
        scratch_shapes=[
            pltpu.VMEM((2, rows, cols), f32),
            pltpu.VMEM((patches, size, size), bf16),
            pltpu.VMEM((prows, size), f32),
            pltpu.VMEM((prows, prows), bf16),
            pltpu.VMEM((prows, prows), bf16),
            pltpu.VMEM((2, rows, cols), f32),
            pltpu.VMEM((patches, 2, size, size), f32),
            pltpu.VMEM((prows, patches * size), bf16),
            pltpu.VMEM((patches * size, prows), bf16),
            pltpu.VMEM((n, 2, rows // n, cols), f32),
            pltpu.VMEM((n, 2, rows // n, cols), f32),
            pltpu.VMEM((2, rows, cols), f32),
            pltpu.VMEM((cols, cols), f32),
            pltpu.SemaphoreType.DMA((6,)),
        ]
        + [pltpu.SemaphoreType.DMA((CHUNKS,))] * 4
        + Reduction.scratch(n, prows, size) * ITERS,
        compiler_params=pltpu.CompilerParams(
            collective_id=0, has_side_effects=True, vmem_limit_bytes=48 * 1024 * 1024
        ),
    )(
        positions, angle_list, object_init.reshape(2, rows, cols), measured.reshape(patches, size, size),
        probe.reshape(prows, size), jnp.asarray(forward), jnp.asarray(inverse), radial.reshape(cols, cols),
        jnp.asarray(np.cos(phase) * scale), jnp.asarray(np.sin(phase) * scale),
    )
    return slices.reshape(object_init.shape), probe_out.reshape(probe.shape)


def tables(count, index_list):
    cosine_part, sine_part = tables_exact(count, index_list)
    return (cosine_part.astype(jnp.bfloat16), sine_part.astype(jnp.bfloat16))


def left(table, field):
    return jnp.einsum("jk,nkl->njl", table, field, preferred_element_type=jnp.float32)


def right(field, table):
    return jnp.einsum("njk,kl->njl", field, table, preferred_element_type=jnp.float32)


def gradient_list(
    object_field, measured_intensity, scan_positions, probe_field, cosine_theta, sine_theta
):
    size = probe_field.shape[1]
    zero_index = jnp.zeros((), jnp.int32)
    pieces = jax.vmap(
        lambda row, col: lax.dynamic_slice(object_field, (zero_index, row, col), (2, size, size))
    )(scan_positions[:, 0], scan_positions[:, 1])
    piece_re, piece_im = (pieces[:, 0], pieces[:, 1])
    probe_re, probe_im = (probe_field[0], probe_field[1])
    wave_re = (probe_re * piece_re - probe_im * piece_im).astype(jnp.bfloat16)
    wave_im = (probe_re * piece_im + probe_im * piece_re).astype(jnp.bfloat16)
    half_re = (left(cosine_theta, wave_re) + left(sine_theta, wave_im)).astype(jnp.bfloat16)
    half_im = (left(cosine_theta, wave_im) - left(sine_theta, wave_re)).astype(jnp.bfloat16)
    farfield_real = right(half_re, cosine_theta) + right(half_im, sine_theta)
    farfield_imaginary = right(half_im, cosine_theta) - right(half_re, sine_theta)
    residual_error = (
        farfield_real * farfield_real
        + farfield_imaginary * farfield_imaginary
        - measured_intensity.astype(jnp.float32)
    )
    push_re = (residual_error * farfield_real).astype(jnp.bfloat16)
    push_im = (residual_error * farfield_imaginary).astype(jnp.bfloat16)
    back_re = (left(cosine_theta, push_re) - left(sine_theta, push_im)).astype(jnp.bfloat16)
    back_im = (left(cosine_theta, push_im) + left(sine_theta, push_re)).astype(jnp.bfloat16)
    grad_re = right(back_re, cosine_theta) - right(back_im, sine_theta)
    grad_im = right(back_im, cosine_theta) + right(back_re, sine_theta)
    step_re = probe_re * grad_re + probe_im * grad_im
    step_im = probe_re * grad_im - probe_im * grad_re
    steps_all = jnp.stack([step_re, step_im], 1)

    def place(index, total):
        start = (zero_index, scan_positions[index, 0], scan_positions[index, 1])
        current = lax.dynamic_slice(total, start, (2, size, size))
        return lax.dynamic_update_slice(total, current + steps_all[index], start)

    obj_grad = lax.fori_loop(0, scan_positions.shape[0], place, jnp.zeros_like(object_field))
    pg_re = jnp.sum(piece_re * grad_re + piece_im * grad_im, 0)
    pg_im = jnp.sum(piece_re * grad_im - piece_im * grad_re, 0)
    energy = jnp.sum(piece_re * piece_re + piece_im * piece_im)
    return (obj_grad, jnp.stack([pg_re, pg_im], 0), energy)


def angular(block, wave_cos, wave_sin):
    count = block.shape[0]
    flat = block.reshape(count, -1)
    exact = lax.Precision.HIGHEST
    part_cos = jnp.dot(wave_cos, flat, precision=exact, preferred_element_type=jnp.float32).reshape(
        block.shape
    )
    part_sin = jnp.dot(wave_sin, flat, precision=exact, preferred_element_type=jnp.float32).reshape(
        block.shape
    )
    harm_re = part_cos[:, 0] + part_sin[:, 1]
    harm_im = part_cos[:, 1] - part_sin[:, 0]
    return jnp.stack([harm_re, harm_im], 1)


def plain_device(object_init, measured, positions, angle_list, probe, radial):
    size = probe.shape[1]
    cosine_theta, sine_theta = tables(size, jnp.arange(size, dtype=jnp.int32))
    object_field = object_init
    probe_field = probe
    for step in range(ITERS):

        def one(items):
            return gradient_list(
                items[0], items[1], items[2], probe_field, cosine_theta, sine_theta
            )

        obj_grads, probe_grads, energies = lax.map(one, (object_field, measured, positions))
        probe_total, energy_total = lax.psum((jnp.sum(probe_grads, 0), jnp.sum(energies)), "angle")
        peak = jnp.max(probe_field[0] * probe_field[0] + probe_field[1] * probe_field[1])
        object_field = object_field - object_rate / peak * obj_grads
        probe_field = probe_field - probe_rate * probe_total / (energy_total / (size * size))
    wave_cos, wave_sin = tables_exact(angle_list.shape[0], angle_list)
    gathered = lax.all_to_all(object_field, "angle", split_axis=2, concat_axis=0, tiled=True)
    harm = lax.all_to_all(
        angular(gathered, wave_cos, wave_sin), "angle", split_axis=0, concat_axis=2, tiled=True
    )
    slices = jnp.einsum(
        "kcrn,knm->kcrm",
        harm,
        radial,
        precision=lax.Precision.HIGHEST,
        preferred_element_type=jnp.float32,
    )
    return (slices, probe_field)


def on_device(n, object_init, measured, positions, angle_list, probe, radial):
    rows, cols = object_init.shape[2:]
    patches, size = measured.shape[1:3]
    fits = (
        object_init.shape[0] == 1
        and radial.shape[0] == 1
        and angle_list.shape[0] == n
        and rows == size == LANES
        and cols % (LANES * CHUNKS) == 0
        and patches == 2 * cols // size - 1
        and rows % (n * SUBLANES) == 0
    )
    device = functools.partial(whole_call, n) if fits else plain_device
    return device(object_init, measured, positions, angle_list, probe, radial)


def solution(mesh):
    in_specs = (
        P(("scan", "angle"), None, None, None),
        P(("scan", "angle"), None, None, None),
        P(("scan", "angle"), None, None),
        P("scan"),
        P("scan", None, None),
        P("angle", None, None),
    )
    out_specs = (P(("scan", "angle"), None, None, None), P("scan", None, None))
    return jax.shard_map(
        functools.partial(on_device, mesh.shape["angle"]),
        mesh=mesh, in_specs=in_specs, out_specs=out_specs, check_vma=False,
    )
```

profile of v0, /device:TPU:0, one launch (start us, length us, event | category | flops | bytes accessed | tf_op | source)
XLA Modules:
  0.0 85.0 jit_solution(9456558208192067088)
XLA Ops:
  0.6 0.8 copy.12.pos_ref
  1.4 0.0 copy-start
  1.4 1.2 %copy-done = f32[1,2,128,1024]{3,2,1,0:T(8,128)S(1)} copy-done((f32[1,2,128,1024]{3,2,1,0:T(8,128)S(1)}, f32[1,2,128,1024]{3,2,1,0:T(8,128)}, u32[]{:S(2)}) %copy-start) | copy-done | bytes 1048600
  2.6 0.0 copy-start.1
  2.6 1.0 %copy-done.1 = bf16[1,15,128,128]{3,2,1,0:T(8,128)(2,1)S(1)} copy-done((bf16[1,15,128,128]{3,2,1,0:T(8,128)(2,1)S(1)}, bf16[1,15,128,128]{3,2,1,0:T(8,128)(2,1)}, u32[]{:S(2)}) %copy-start.1) | copy-done | bytes 491544
  3.7 0.0 copy-start.2
  3.7 0.9 %copy-done.2 = f32[2,128,128]{2,1,0:T(8,128)S(1)} copy-done((f32[2,128,128]{2,1,0:T(8,128)S(1)}, f32[2,128,128]{2,1,0:T(8,128)}, u32[]{:S(2)}) %copy-start.2) | copy-done | bytes 131096
  4.6 0.0 copy-start.3
  4.6 0.9 %copy-done.3 = bf16[256,256]{1,0:T(8,128)(2,1)S(1)} copy-done((bf16[256,256]{1,0:T(8,128)(2,1)S(1)}, bf16[256,256]{1,0:T(8,128)(2,1)}, u32[]{:S(2)}) %copy-start.3) | copy-done | bytes 131096
  5.5 0.0 copy-start.4
  5.5 0.9 %copy-done.4 = bf16[256,256]{1,0:T(8,128)(2,1)S(1)} copy-done((bf16[256,256]{1,0:T(8,128)(2,1)S(1)}, bf16[256,256]{1,0:T(8,128)(2,1)}, u32[]{:S(2)}) %copy-start.4) | copy-done | bytes 131096
  6.4 0.0 copy-start.5
  6.4 0.7 copy-done.5
  7.0 0.0 copy-start.6
  7.0 0.7 copy-done.6
  7.7 0.0 copy-start.7
  7.7 0.7 copy-done.7
  8.3 75.0 %whole.1 = (f32[256,1024]{1,0:T(8,128)S(1)}, f32[256,128]{1,0:T(8,128)S(1)}) custom-call(s32[1,15,2]{2,1,0:T(8,128)S(1)} %copy.12.pos_ref, s32[16]{0:T(128)S(1)} %copy-done.5, f32[2,128,1024]{2,1,0:T(8,128)S(1)} %bitcast.7, bf16[15,128,128]{2,1,0:T(8,128)(2,1)S(1)} %bitcast.8, f32[256,128]{1,0:T(8,128)S(1)} %bitcast.9, bf16[256,256]{1,0:T(8,128)(2,1)S(1)} %copy-done.4, ...), custom_call_target="tpu_custom_call" | custom-call | tf_op jit(solution)/shard_map/whole/pallas_call | solution.py:312
  83.4 1.0 %copy.15 = f32[1,2,128,1024]{3,2,1,0:T(8,128)} copy(f32[1,2,128,1024]{3,2,1,0:T(8,128)S(1)} %bitcast.6) | data formatting | bytes 2097152
  84.3 0.7 copy.16
Async XLA Ops:
  1.4 1.2 %copy-start = (f32[1,2,128,1024]{3,2,1,0:T(8,128)S(1)}, f32[1,2,128,1024]{3,2,1,0:T(8,128)}, u32[]{:S(2)}) copy-start(f32[1,2,128,1024]{3,2,1,0:T(8,128)} %param.10) | copy-start | bytes 3145732
  2.6 1.0 %copy-start.1 = (bf16[1,15,128,128]{3,2,1,0:T(8,128)(2,1)S(1)}, bf16[1,15,128,128]{3,2,1,0:T(8,128)(2,1)}, u32[]{:S(2)}) copy-start(bf16[1,15,128,128]{3,2,1,0:T(8,128)(2,1)} %param.11) | copy-start | bytes 1474564
  3.7 0.9 %copy-start.2 = (f32[2,128,128]{2,1,0:T(8,128)S(1)}, f32[2,128,128]{2,1,0:T(8,128)}, u32[]{:S(2)}) copy-start(f32[2,128,128]{2,1,0:T(8,128)} %param.14) | copy-start | bytes 393220
  4.6 0.9 %copy-start.3 = (bf16[256,256]{1,0:T(8,128)(2,1)S(1)}, bf16[256,256]{1,0:T(8,128)(2,1)}, u32[]{:S(2)}) copy-start(bf16[256,256]{1,0:T(8,128)(2,1)} %constant.9.clone.inv_hbm) | copy-start | bytes 393220
  5.5 0.9 %copy-start.4 = (bf16[256,256]{1,0:T(8,128)(2,1)S(1)}, bf16[256,256]{1,0:T(8,128)(2,1)}, u32[]{:S(2)}) copy-start(bf16[256,256]{1,0:T(8,128)(2,1)} %constant.8.clone.fwd_hbm) | copy-start | bytes 393220
  6.4 0.7 copy-start.5
  7.0 0.7 copy-start.6
  7.7 0.7 copy-start.7
where the time goes:
time: 85.3 us; the launch traced here: 85 us
  Pallas kernels  75 us (88%)
  local copies, waits for them, and re-layouts  9.32 us (11%)
    pallas_call x1, Pallas kernels, whole_call(): pl.pallas_call(functools.partial(whole_kernel, n), name='whole', out_shap...  75 us
    unnamed x19, local copies, waits for them, and re-layouts  9.32 us

commit v1 on v0

--- a/solution.py
+++ b/solution.py
@@ -11,6 +11,7 @@
 
 ITERS = 2
 CHUNKS = 4
+GROUP = 4
 LANES = 128
 SUBLANES = 8
 
@@ -19,7 +20,7 @@
 
 VMEM_SPEC = pl.BlockSpec(memory_space=pltpu.VMEM)
 SMEM_SPEC = pl.BlockSpec(memory_space=pltpu.SMEM)
-ANY_SPEC = pl.BlockSpec(memory_space=pl.ANY)
+HBM_SPEC = pl.BlockSpec(memory_space=pltpu.HBM)
 
 
 def tables_exact(count, index_list):
@@ -69,6 +70,19 @@
         return carry
 
     lax.fori_loop(1, n, one, 0)
+
+
+def send_along(count, mine, peer, make):
+    def one(i, carry):
+        j = lax.rem(mine + i, count)
+        src, dst, send_sem, recv_sem = make(j)
+        pltpu.make_async_remote_copy(
+            src_ref=src, dst_ref=dst, send_sem=send_sem, recv_sem=recv_sem,
+            device_id={"angle": peer(j)}, device_id_type=pl.DeviceIdType.MESH,
+        ).start()
+        return carry
+
+    lax.fori_loop(1, count, one, 0)
 
 
 def drain(ref, sem):
@@ -198,11 +212,100 @@
         drain(self.full.at[pl.ds(0, (n - 1) * self.share)], sems.at[4])
 
 
+class Nested:
+    def __init__(self, n, me, pg, en, got_a, en_a, part, en_part, got_b, en_b, full, sems):
+        self.g, self.m = GROUP, n // GROUP
+        self.u, self.z = lax.rem(me, GROUP), me // GROUP
+        self.pg, self.en, self.full, self.sems = pg, en, full, sems
+        self.got_a, self.en_a, self.part, self.en_part = got_a, en_a, part, en_part
+        self.got_b, self.en_b = got_b, en_b
+        self.coarse, self.fine = pg.shape[0] // GROUP, pg.shape[0] // n
+
+    @staticmethod
+    def scratch(n, rows, size):
+        f32, m = jnp.float32, n // GROUP
+        return [
+            pltpu.VMEM((rows, size), f32),
+            pltpu.VMEM((1, size), f32),
+            pltpu.VMEM((GROUP, rows // GROUP, size), f32),
+            pltpu.VMEM((GROUP, 1, size), f32),
+            pltpu.VMEM((rows // GROUP, size), f32),
+            pltpu.VMEM((1, size), f32),
+            pltpu.VMEM((m, rows // n, size), f32),
+            pltpu.VMEM((m, 1, size), f32),
+            pltpu.VMEM((rows, size), f32),
+            pltpu.SemaphoreType.DMA((12,)),
+        ]
+
+    def near(self, j):
+        return self.z * self.g + j
+
+    def across(self, j):
+        return j * self.g + self.u
+
+    def mine(self):
+        return pl.ds(pl.multiple_of(self.u * self.coarse + self.z * self.fine, SUBLANES), self.fine)
+
+    def scatter(self):
+        g, u, sems = self.g, self.u, self.sems
+        send_along(g, u, self.near, lambda j: (
+            self.pg.at[rows_at(j, self.coarse)], self.got_a.at[u], sems.at[0], sems.at[1]
+        ))
+        send_along(g, u, self.near, lambda j: (self.en, self.en_a.at[u], sems.at[2], sems.at[3]))
+        self.got_a[u] = self.pg[rows_at(u, self.coarse), :]
+        self.en_a[u] = self.en[...]
+
+    def cross(self):
+        g, m, z, sems = self.g, self.m, self.z, self.sems
+        drain(self.got_a.at[pl.ds(0, g - 1)], sems.at[1])
+        drain(self.en_a.at[pl.ds(0, g - 1)], sems.at[3])
+        self.part[...] = jnp.sum(self.got_a[...], 0)
+        self.en_part[...] = jnp.sum(self.en_a[...], 0)
+        send_along(m, z, self.across, lambda j: (
+            self.part.at[rows_at(j, self.fine)], self.got_b.at[z], sems.at[4], sems.at[5]
+        ))
+        send_along(m, z, self.across, lambda j: (self.en_part, self.en_b.at[z], sems.at[6], sems.at[7]))
+        self.got_b[z] = self.part[rows_at(z, self.fine), :]
+        self.en_b[z] = self.en_part[...]
+
+    def gather(self, probe):
+        m, z, sems, mine = self.m, self.z, self.sems, self.mine()
+        drain(self.got_b.at[pl.ds(0, m - 1)], sems.at[5])
+        drain(self.en_b.at[pl.ds(0, m - 1)], sems.at[7])
+        size = probe.shape[1]
+        total = jnp.sum(self.got_b[...], 0)
+        energy = jnp.sum(self.en_b[...])
+        self.full[mine, :] = probe[mine, :] - probe_rate * total / (energy / (size * size))
+        send_along(m, z, self.across, lambda j: (
+            self.full.at[mine], self.full.at[mine], sems.at[8], sems.at[9]
+        ))
+
+    def share(self):
+        g, m, u, sems = self.g, self.m, self.u, self.sems
+        drain(self.full.at[pl.ds(0, (m - 1) * self.fine)], sems.at[9])
+        rows = rows_at(u, self.coarse)
+        send_along(g, u, self.near, lambda j: (
+            self.full.at[rows], self.full.at[rows], sems.at[10], sems.at[11]
+        ))
+
+    def arrive(self):
+        drain(self.full.at[pl.ds(0, (self.g - 1) * self.coarse)], self.sems.at[11])
+
+    def leave(self):
+        g, m, sems = self.g, self.m, self.sems
+        drain(self.got_a.at[pl.ds(0, g - 1)], sems.at[0])
+        drain(self.en_a.at[pl.ds(0, g - 1)], sems.at[2])
+        drain(self.got_b.at[pl.ds(0, m - 1)], sems.at[4])
+        drain(self.en_b.at[pl.ds(0, m - 1)], sems.at[6])
+        drain(self.full.at[pl.ds(0, (m - 1) * self.fine)], sems.at[8])
+        drain(self.full.at[pl.ds(0, (g - 1) * self.coarse)], sems.at[10])
+
+
 def whole_kernel(
-    n, pos_ref, ang_ref, obj_hbm, meas_hbm, prb_hbm, fwd_hbm, inv_hbm, radial_hbm, cos_ref, sin_ref,
+    n, pos_ref, ang_ref, obj_hbm, meas_hbm, prb_hbm, fwd_hbm, inv_hbm, radial_hbm, wave_ref,
     out_ref, probe_ref,
     obj, meas, prb, fwd, inv, acc, piece, wave, mid,
-    got, spread, harm, matrix, load_sems, send_a, recv_a, send_b, recv_b, *reds,
+    got, spread, harm, matrix, high, low, load_sems, send_a, recv_a, send_b, recv_b, *reds,
 ):
     me = lax.axis_index("angle")
     rows, cols = obj.shape[1:]
@@ -228,10 +331,13 @@
     spans = [pl.ds(q * wide, wide) for q in range(CHUNKS)]
     ends = [min(patches, 2 * (wide // size) * (q + 1) + 1) for q in range(CHUNKS)]
     groups = list(zip([0] + ends[:-1], ends))
-    each = len(reds) // ITERS
+    many = len(Reduction.scratch(n, 2 * size, size))
     probe = prb
     for step in range(ITERS):
-        red = Reduction(n, me, *reds[step * each:(step + 1) * each])
+        if step < ITERS - 1:
+            red = Reduction(n, me, *reds[step * many:(step + 1) * many])
+        else:
+            red = Nested(n, me, *reds[step * many:])
         pre, pim = probe[:size, :], probe[size:, :]
         rate = object_rate / jnp.max(pre * pre + pim * pim)
         energy = jnp.zeros((SUBLANES, size), jnp.float32)
@@ -242,33 +348,48 @@
             span = spans[q]
             obj[:, :, span] = obj[:, :, span] - rate * acc[:, :, span]
             acc[:, :, span] = jnp.zeros((2, rows, wide), jnp.float32)
+            if q == CHUNKS - 1:
+                red.en[...] = jnp.sum(energy, 0, keepdims=True)
+                if step == 0:
+                    pl.semaphore_wait(pltpu.get_barrier_semaphore(), n - 1)
+                red.scatter()
             if step == ITERS - 1:
                 send(n, me, lambda d: (
                     obj.at[:, rows_at(d, share), span], got.at[me, :, :, span], send_a.at[q], recv_a.at[q]
                 ))
-        red.en[...] = jnp.sum(energy, 0, keepdims=True)
-        if step == 0:
-            pl.semaphore_wait(pltpu.get_barrier_semaphore(), n - 1)
-        red.scatter()
         if step < ITERS - 1:
             red.gather(probe)
             red.arrive()
             red.leave()
             probe = red.full
     got[me] = obj[:, rows_at(me, share), :]
-    red.gather(probe)
-
-    def weight(ref, k, b):
-        return ref[lax.rem(k * ang_ref[b], n)]
+    red.cross()
+    loads[-1].wait()
+
+    def split(i, carry):
+        part = pl.ds(pl.multiple_of(i * LANES, LANES), LANES)
+        value = matrix[part, :]
+        top = value.astype(jnp.bfloat16)
+        high[part, :] = top
+        low[part, :] = (value - top.astype(jnp.float32)).astype(jnp.bfloat16)
+        return carry
+
+    lax.fori_loop(0, cols // LANES, split, 0)
+
+    def weights(k, b):
+        phase = lax.rem(k * ang_ref[b], n)
+        return wave_ref[phase], wave_ref[phase + n]
 
     for q, span in enumerate(spans):
         drain(got.at[pl.ds(0, n - 1), :, :, span], recv_a.at[q])
+        if q == CHUNKS - 1:
+            red.gather(probe)
 
         def harmonic(k, carry):
             re = jnp.zeros((share, wide), jnp.float32)
             im = jnp.zeros((share, wide), jnp.float32)
             for b in range(n):
-                wc, ws = weight(cos_ref, k, b), weight(sin_ref, k, b)
+                wc, ws = weights(k, b)
                 pr, pi = got[b, 0, :, span], got[b, 1, :, span]
                 re += wc * pr + ws * pi
                 im += wc * pi - ws * pr
@@ -281,20 +402,20 @@
             spread.at[d, :, :, span], harm.at[:, rows_at(me, share), span], send_b.at[q], recv_b.at[q]
         ))
         harm[:, rows_at(me, share), span] = spread[me, :, :, span]
-    loads[-1].wait()
     for q, span in enumerate(spans):
         drain(harm.at[:, pl.ds(0, (n - 1) * share), span], recv_b.at[q])
-        part = jnp.dot(
-            harm[:, :, span].reshape(2 * rows, wide), matrix[span, :],
-            precision=lax.Precision.HIGHEST, preferred_element_type=jnp.float32,
-        )
+        value = harm[:, :, span].reshape(2 * rows, wide)
+        top = value.astype(jnp.bfloat16)
+        rest = (value - top.astype(jnp.float32)).astype(jnp.bfloat16)
+        part = dot32(rest, high[span, :]) + dot32(top, low[span, :]) + dot32(top, high[span, :])
         if q == 0:
             out_ref[...] = part
         else:
             out_ref[...] += part
         if q == CHUNKS - 2:
-            red.arrive()
-            probe_ref[...] = red.full[...]
+            red.share()
+    red.arrive()
+    probe_ref[...] = red.full[...]
     red.leave()
     for q, span in enumerate(spans):
         drain(got.at[pl.ds(0, n - 1), :, :, span], send_a.at[q])
@@ -316,7 +437,7 @@
             jax.ShapeDtypeStruct((2 * rows, cols), f32),
             jax.ShapeDtypeStruct((prows, size), f32),
         ),
-        in_specs=[SMEM_SPEC] * 2 + [ANY_SPEC] * 6 + [SMEM_SPEC] * 2,
+        in_specs=[SMEM_SPEC] * 2 + [HBM_SPEC] * 6 + [SMEM_SPEC],
         out_specs=(VMEM_SPEC,) * 2,
         scratch_shapes=[
             pltpu.VMEM((2, rows, cols), f32),
@@ -332,17 +453,20 @@
             pltpu.VMEM((n, 2, rows // n, cols), f32),
             pltpu.VMEM((2, rows, cols), f32),
             pltpu.VMEM((cols, cols), f32),
+            pltpu.VMEM((cols, cols), bf16),
+            pltpu.VMEM((cols, cols), bf16),
             pltpu.SemaphoreType.DMA((6,)),
         ]
         + [pltpu.SemaphoreType.DMA((CHUNKS,))] * 4
-        + Reduction.scratch(n, prows, size) * ITERS,
+        + Reduction.scratch(n, prows, size) * (ITERS - 1)
+        + Nested.scratch(n, prows, size),
         compiler_params=pltpu.CompilerParams(
-            collective_id=0, has_side_effects=True, vmem_limit_bytes=48 * 1024 * 1024
+            collective_id=0, has_side_effects=True, vmem_limit_bytes=67043328
         ),
     )(
         positions, angle_list, object_init.reshape(2, rows, cols), measured.reshape(patches, size, size),
         probe.reshape(prows, size), jnp.asarray(forward), jnp.asarray(inverse), radial.reshape(cols, cols),
-        jnp.asarray(np.cos(phase) * scale), jnp.asarray(np.sin(phase) * scale),
+        jnp.asarray(np.concatenate([np.cos(phase), np.sin(phase)]) * scale),
     )
     return slices.reshape(object_init.shape), probe_out.reshape(probe.shape)
 
@@ -461,6 +585,8 @@
         and cols % (LANES * CHUNKS) == 0
         and patches == 2 * cols // size - 1
         and rows % (n * SUBLANES) == 0
+        and n % GROUP == 0
+        and n > GROUP
     )
     device = functools.partial(whole_call, n) if fits else plain_device
     return device(object_init, measured, positions, angle_list, probe, radial)

time: 85.3 us -> 77.1 us (0.904)
  local copies, waits for them, and re-layouts: 9.32 us -> 5.23 us
  Pallas kernels: 75 us -> 71 us
    unnamed x19 -> x3, local copies, waits for them, and re-layouts: 9.32 us -> 5.23 us
    pallas_call x1, Pallas kernels: 75 us -> 71 us  [whole_call(): pl.pallas_call(functools.partial(whole_kernel, n), name='whole', out_shap...]
where the time goes in v1:
time: 77.1 us; the launch traced here: 76.9 us
  Pallas kernels  71 us (92%)
  local copies, waits for them, and re-layouts  5.23 us (7%)
    pallas_call x1, Pallas kernels, whole_call(): pl.pallas_call(functools.partial(whole_kernel, n), name='whole', out_shap...  71 us
    unnamed x3, local copies, waits for them, and re-layouts  5.23 us

profile of v1, /device:TPU:0, one launch (start us, length us, event | category | flops | bytes accessed | tf_op | source)
XLA Modules:
  0.0 76.9 jit_solution(12626605352417737611)
XLA Ops:
  0.6 1.4 %copy.11.pos_ref = s32[1,15,2]{2,1,0:T(8,128)} copy(s32[1,15,2]{1,2,0:T(2,128)} %param.11) | data formatting | bytes 240 | tf_op args[2]
  2.0 71.0 %whole.1 = (f32[256,1024]{1,0:T(8,128)}, f32[256,128]{1,0:T(8,128)}) custom-call(s32[1,15,2]{2,1,0:T(8,128)} %copy.11.pos_ref, s32[16]{0:T(128)} %ang_ref.1, f32[2,128,1024]{2,1,0:T(8,128)} %bitcast.7, bf16[15,128,128]{2,1,0:T(8,128)(2,1)} %bitcast.9, f32[256,128]{1,0:T(8,128)} %bitcast.10, bf16[256,256]{1,0:T(8,128)(2,1)} %constant.6.clone.fwd_hbm, ...), custom_call_target="tpu_custom_call" | custom-call | tf_op jit(solution)/shard_map/whole/pallas_call | solution.py:433
  73.0 2.3 %copy.14 = f32[1,2,128,1024]{3,2,1,0:T(8,128)} copy(f32[1,2,128,1024]{3,2,1,0:T(8,128)} %bitcast.8) | data formatting | bytes 2097152
  75.3 1.6 %copy.15 = f32[2,128,128]{2,1,0:T(8,128)} copy(f32[2,128,128]{2,1,0:T(8,128)} %bitcast.11) | data formatting | bytes 262144
